TPU v7x, 8 devices: a whole 2x2x1 slice. The times are simulated.
8 devices in a mesh: data: 1 (over z), row: 2 (over y), col: 2 (over x), core: 2 (over core).
Axes of the slice: x: 2, y: 2, z: 1, core: 2. Of those that a mesh axis runs over, the one named last changes fastest.
Arguments:
- tokens: bfloat16 [2, 1024, 2048], P('data', ('row', 'col', 'core'))
- w_qkv: bfloat16 [2048, 3, 32, 64], replicated
- w_out: bfloat16 [32, 64, 2048], replicated
Outputs:
- output: bfloat16 [2, 1024, 2048], P('data', ('row', 'col', 'core'))
All inputs are finite; a program needn't handle non-finite values.
Results may differ from a plain program's by a relative error of at most 0.00747195.
Values are sent between devices in bfloat16 or wider.
A program may use at most 1 GiB of HBM per device.

v0:
```python
import jax
import jax.numpy as jnp
from jax import lax
from jax.sharding import PartitionSpec as P


def init_state(queries):
    batch_n, query_n, head_n, head_dim = queries.shape
    run_max = jnp.full((batch_n, head_n, query_n), -jnp.inf, jnp.float32)
    run_acc = jnp.zeros((batch_n, head_n, query_n, head_dim), jnp.float32)
    return run_max, jnp.zeros_like(run_max), run_acc


def attend_keys(queries, kv_rows, state):
    blk_len = min(128, kv_rows.shape[1])
    logit_scale = queries.shape[-1] ** -0.5

    def key_step(blk_index, run_state):
        run_max, run_sum, run_acc = run_state
        kv_piece = lax.dynamic_slice_in_dim(kv_rows, blk_index * blk_len, blk_len, axis=1)
        scores = jnp.einsum("bqhd,bkhd->bhqk", queries, kv_piece[:, :, 0], preferred_element_type=jnp.float32) * logit_scale
        new_max = jnp.maximum(run_max, jnp.max(scores, axis=-1))
        rescale = jnp.exp(run_max - new_max)
        weights = jnp.exp(scores - new_max[..., None])
        run_sum = run_sum * rescale + jnp.sum(weights, axis=-1)
        run_acc = run_acc * rescale[..., None] + jnp.einsum("bhqk,bkhd->bhqd", weights.astype(jnp.bfloat16), kv_piece[:, :, 1], preferred_element_type=jnp.float32)
        return new_max, run_sum, run_acc

    return lax.fori_loop(0, kv_rows.shape[1] // blk_len, key_step, state)


def finish_state(state):
    run_sum = state[1]
    run_acc = state[2]
    attn_out = (run_acc / run_sum[..., None]).astype(jnp.bfloat16)
    return jnp.transpose(attn_out, (0, 2, 1, 3))


def solution(mesh):
    head_axes = ("col", "core")
    tok_spec = P("data", ("row", "col", "core"), None)

    def per_device(tokens, w_qkv, w_out):
        qkv_loc = jnp.einsum("btc,cjhd->btjhd", tokens, w_qkv, preferred_element_type=jnp.float32).astype(jnp.bfloat16)
        qkv_grp = lax.all_to_all(qkv_loc, head_axes, 3, 1, tiled=True)
        queries = qkv_grp[:, :, 0]
        kv_all = lax.all_gather(qkv_grp[:, :, 1:], "row", axis=1, tiled=True)
        attn_out = finish_state(attend_keys(queries, kv_all, init_state(queries)))
        attn_loc = lax.all_to_all(attn_out, head_axes, 1, 2, tiled=True)
        return jnp.einsum("bthd,hdc->btc", attn_loc, w_out, preferred_element_type=jnp.float32).astype(jnp.bfloat16)

    return jax.shard_map(per_device, mesh=mesh, in_specs=(tok_spec, P(), P()), out_specs=tok_spec, check_vma=False)
```

profile of v0, /device:TPU:0, one launch (start us, length us, event | category | flops | bytes accessed | tf_op | source)
XLA Modules:
  0.0 214.0 jit_solution(15779919306632019005)
XLA Ops:
  6.5 1.2 copy-done
  7.8 11.6 %fusion.25 = bf16[2,128,3,32,64]{1,4,3,2,0:T(8,128)(2,1)S(1)} fusion(bf16[2048,3,32,64]{0,3,2,1:T(8,128)(2,1)} %param.6, bf16[2,128,2048]{2,1,0:T(8,128)(2,1)S(1)} %copy-done), kind=kOutput, calls=%fused_computation.27 | convolution fusion | flops 6444023808 | bytes 29360128 | tf_op jit(solution)/shard_map/btc,cjhd->btjhd/dot_general | solution.py:44
  20.0 41.3 %all_to_all.36 = bf16[2,128,3,32,64]{1,4,2,0,3:T(8,128)(2,1)S(1)} all-to-all(bf16[2,128,3,32,64]{1,4,2,0,3:T(8,128)(2,1)S(1)} %copy.8), channel_id=1, replica_groups=mesh['data'=1,'row'=2,'col'=2,'core'=2] {'col','core'}, dimensions={3} | all-to-all | bytes 6291456 | tf_op jit(solution)/shard_map/all_to_all | solution.py:45
  61.4 4.7 %copy.9 = bf16[2,4,128,3,8,64]{2,1,5,4,0,3:T(4,128)(2,1)} copy(bf16[2,4,128,3,8,64]{2,5,3,0,4,1:T(8,128)(2,1)S(1)} %bitcast.74) | data formatting | bytes 6291456 | tf_op jit(solution)/shard_map/all_to_all | solution.py:45
  66.0 5.7 %all_to_all.29 = bf16[2,512,3,8,64]{1,4,3,0,2:T(8,128)(2,1)} reshape(bf16[2,4,128,3,8,64]{2,1,5,4,0,3:T(4,128)(2,1)} %copy.9) | data formatting | bytes 6291456 | tf_op jit(solution)/shard_map/all_to_all | solution.py:45
  71.8 3.2 %slice.24 = bf16[2,512,2,8,64]{1,4,3,0,2:T(8,128)(2,1)} slice(bf16[2,512,3,8,64]{1,4,3,0,2:T(8,128)(2,1)} %all_to_all.29), slice={[0:2], [0:512], [1:3], [0:8], [0:64]} | slice | bytes 4194304 | tf_op jit(solution)/shard_map/slice | solution.py:47
  75.0 1.3 slice_bitcast_fusion
  76.3 53.0 %all-gather.2.cloned.1.call-done = bf16[2,1024,2,8,64]{1,4,3,0,2:T(8,128)(2,1)} async-done(((bf16[2,512,2,8,64]{1,4,3,0,2:T(8,128)(2,1)}), bf16[2,1024,2,8,64]{1,4,3,0,2:T(8,128)(2,1)}) %all-gather.2.cloned.1.call-update) | async-done | bytes 4194320 | tf_op jit(solution)/shard_map/all_gather | solution.py:47
  129.4 39.5 %while.18 = (s32[]{:T(128)}, f32[2,8,512]{2,1,0:T(8,128)S(1)}, f32[2,8,512]{2,1,0:T(8,128)S(1)}, f32[2,8,512,64]{2,3,1,0:T(8,128)S(1)}, bf16[2,1024,2,8,64]{1,4,...) while((s32[]{:T(128)}, f32[2,8,512]{2,1,0:T(8,128)S(1)}, ...), condition=%wide.region_3.0_spmd.clone, body=%wide.region_0.0_spmd.clone.sunk | while | flops 278437888 | bytes 18874568 | solution.py:29
  129.4 1.7 bitcast_reduce_fusion.2
  131.9 2.4 %fusion.42 = f32[2,8,512,64]{2,3,1,0:T(8,128)S(1)} fusion(f32[2,8,512,64]{2,3,1,0:T(8,128)S(1)} %get-tuple-element.213, f32[2,8,128,512]{3,2,1,0:T(8,128)S(1)} %get-tuple-element.196, f32[2,8,512]{2,1,0:T(8,128)S(1)} %select_maximum_fusion.2, f32[2,8,512]{2,1,0:T(8,128)S(1)} %get-tuple-element.198, pred[]{:T(512)S(6)} %compare.3, ...), kind=kOutput, calls=%fused_computation.7.clone.1 | convolution fusion | flops 138936320 | bytes 8716297 | tf_op jit(solution)/shard_map/while/body/eval_jaxpr/bhqk,bkhd->bhqd/dot_general | solution.py:26
  134.3 1.7 bitcast_reduce_fusion.2
  136.9 2.4 %fusion.42 = f32[2,8,512,64]{2,3,1,0:T(8,128)S(1)} fusion(f32[2,8,512,64]{2,3,1,0:T(8,128)S(1)} %get-tuple-element.213, f32[2,8,128,512]{3,2,1,0:T(8,128)S(1)} %get-tuple-element.196, f32[2,8,512]{2,1,0:T(8,128)S(1)} %select_maximum_fusion.2, f32[2,8,512]{2,1,0:T(8,128)S(1)} %get-tuple-element.198, pred[]{:T(512)S(6)} %compare.3, ...), kind=kOutput, calls=%fused_computation.7.clone.1 | convolution fusion | flops 138936320 | bytes 8716297 | tf_op jit(solution)/shard_map/while/body/eval_jaxpr/bhqk,bkhd->bhqd/dot_general | solution.py:26
  139.3 1.7 bitcast_reduce_fusion.2
  141.8 2.4 %fusion.42 = f32[2,8,512,64]{2,3,1,0:T(8,128)S(1)} fusion(f32[2,8,512,64]{2,3,1,0:T(8,128)S(1)} %get-tuple-element.213, f32[2,8,128,512]{3,2,1,0:T(8,128)S(1)} %get-tuple-element.196, f32[2,8,512]{2,1,0:T(8,128)S(1)} %select_maximum_fusion.2, f32[2,8,512]{2,1,0:T(8,128)S(1)} %get-tuple-element.198, pred[]{:T(512)S(6)} %compare.3, ...), kind=kOutput, calls=%fused_computation.7.clone.1 | convolution fusion | flops 138936320 | bytes 8716297 | tf_op jit(solution)/shard_map/while/body/eval_jaxpr/bhqk,bkhd->bhqd/dot_general | solution.py:26
  144.2 1.7 bitcast_reduce_fusion.2
  146.7 2.4 %fusion.42 = f32[2,8,512,64]{2,3,1,0:T(8,128)S(1)} fusion(f32[2,8,512,64]{2,3,1,0:T(8,128)S(1)} %get-tuple-element.213, f32[2,8,128,512]{3,2,1,0:T(8,128)S(1)} %get-tuple-element.196, f32[2,8,512]{2,1,0:T(8,128)S(1)} %select_maximum_fusion.2, f32[2,8,512]{2,1,0:T(8,128)S(1)} %get-tuple-element.198, pred[]{:T(512)S(6)} %compare.3, ...), kind=kOutput, calls=%fused_computation.7.clone.1 | convolution fusion | flops 138936320 | bytes 8716297 | tf_op jit(solution)/shard_map/while/body/eval_jaxpr/bhqk,bkhd->bhqd/dot_general | solution.py:26
  149.1 1.7 bitcast_reduce_fusion.2
  151.7 2.4 %fusion.42 = f32[2,8,512,64]{2,3,1,0:T(8,128)S(1)} fusion(f32[2,8,512,64]{2,3,1,0:T(8,128)S(1)} %get-tuple-element.213, f32[2,8,128,512]{3,2,1,0:T(8,128)S(1)} %get-tuple-element.196, f32[2,8,512]{2,1,0:T(8,128)S(1)} %select_maximum_fusion.2, f32[2,8,512]{2,1,0:T(8,128)S(1)} %get-tuple-element.198, pred[]{:T(512)S(6)} %compare.3, ...), kind=kOutput, calls=%fused_computation.7.clone.1 | convolution fusion | flops 138936320 | bytes 8716297 | tf_op jit(solution)/shard_map/while/body/eval_jaxpr/bhqk,bkhd->bhqd/dot_general | solution.py:26
  154.1 1.7 bitcast_reduce_fusion.2
  156.6 2.4 %fusion.42 = f32[2,8,512,64]{2,3,1,0:T(8,128)S(1)} fusion(f32[2,8,512,64]{2,3,1,0:T(8,128)S(1)} %get-tuple-element.213, f32[2,8,128,512]{3,2,1,0:T(8,128)S(1)} %get-tuple-element.196, f32[2,8,512]{2,1,0:T(8,128)S(1)} %select_maximum_fusion.2, f32[2,8,512]{2,1,0:T(8,128)S(1)} %get-tuple-element.198, pred[]{:T(512)S(6)} %compare.3, ...), kind=kOutput, calls=%fused_computation.7.clone.1 | convolution fusion | flops 138936320 | bytes 8716297 | tf_op jit(solution)/shard_map/while/body/eval_jaxpr/bhqk,bkhd->bhqd/dot_general | solution.py:26
  159.0 1.7 bitcast_reduce_fusion.2
  161.5 2.4 %fusion.42 = f32[2,8,512,64]{2,3,1,0:T(8,128)S(1)} fusion(f32[2,8,512,64]{2,3,1,0:T(8,128)S(1)} %get-tuple-element.213, f32[2,8,128,512]{3,2,1,0:T(8,128)S(1)} %get-tuple-element.196, f32[2,8,512]{2,1,0:T(8,128)S(1)} %select_maximum_fusion.2, f32[2,8,512]{2,1,0:T(8,128)S(1)} %get-tuple-element.198, pred[]{:T(512)S(6)} %compare.3, ...), kind=kOutput, calls=%fused_computation.7.clone.1 | convolution fusion | flops 138936320 | bytes 8716297 | tf_op jit(solution)/shard_map/while/body/eval_jaxpr/bhqk,bkhd->bhqd/dot_general | solution.py:26
  163.9 1.7 bitcast_reduce_fusion.2
  166.5 2.4 %fusion.42 = f32[2,8,512,64]{2,3,1,0:T(8,128)S(1)} fusion(f32[2,8,512,64]{2,3,1,0:T(8,128)S(1)} %get-tuple-element.213, f32[2,8,128,512]{3,2,1,0:T(8,128)S(1)} %get-tuple-element.196, f32[2,8,512]{2,1,0:T(8,128)S(1)} %select_maximum_fusion.2, f32[2,8,512]{2,1,0:T(8,128)S(1)} %get-tuple-element.198, pred[]{:T(512)S(6)} %compare.3, ...), kind=kOutput, calls=%fused_computation.7.clone.1 | convolution fusion | flops 138936320 | bytes 8716297 | tf_op jit(solution)/shard_map/while/body/eval_jaxpr/bhqk,bkhd->bhqd/dot_general | solution.py:26
  169.1 3.8 %copy.11 = f32[2,8,512,64]{3,1,0,2:T(8,128)} copy(f32[2,8,512,64]{2,3,1,0:T(8,128)S(1)} %get-tuple-element.115) | data formatting | bytes 4194304 | tf_op jit(solution)/shard_map/while | solution.py:29
  172.9 2.9 %fusion.30 = bf16[512,2,8,64]{3,2,1,0:T(8,128)(2,1)S(1)} fusion(f32[2,8,512,64]{3,1,0,2:T(8,128)} %copy.11, f32[2,8,512]{1,0,2:T(2,128)S(1)} %copy.10), kind=kLoop, calls=%fused_computation.31 | loop fusion | flops 1048576 | bytes 3178496
  175.7 1.7 reshape.7
  177.4 17.5 %all_to_all.37 = bf16[4,2,65536]{2,1,0:T(2,128)(2,1)} all-to-all(bf16[4,2,65536]{2,1,0:T(2,128)(2,1)S(1)} %reshape.7), channel_id=1, replica_groups=mesh['data'=1,'row'=2,'col'=2,'core'=2] {'col','core'}, dimensions={0} | all-to-all | bytes 2097152 | tf_op jit(solution)/shard_map/all_to_all | solution.py:49
  194.9 3.1 %reshape.8 = bf16[512,2,8,64]{3,2,1,0:T(8,128)(2,1)S(1)} reshape(bf16[4,2,65536]{2,1,0:T(2,128)(2,1)} %all_to_all.37) | data formatting | bytes 2097152
  198.0 2.1 copy.12
  200.1 7.1 %fusion.22 = bf16[2,128,2048]{2,1,0:T(8,128)(2,1)} fusion(bf16[2,128,32,64]{1,3,2,0:T(8,128)(2,1)} %bitcast.76, bf16[32,64,2048]{2,1,0:T(8,128)(2,1)} %param.7), kind=kOutput, calls=%fused_computation.26 | convolution fusion | flops 2148007936 | bytes 10485760 | tf_op jit(solution)/shard_map/bthd,hdc->btc/dot_general | solution.py:50
  (42 shorter events, 7.3 us)
Async XLA Ops:
  6.5 1.2 copy-start
  6.5 122.9 %all-gather.2.cloned.1.call-start = ((), (), s32[]{:S(2)}) async-start(), calls=%async_computation.2 | async-start | bytes 6291456 | tf_op jit(solution)/shard_map/all_gather | solution.py:47
  200.1 7.1 %copy-start.1 = (bf16[2,128,2048]{2,1,0:T(8,128)(2,1)S(1)}, bf16[2,128,2048]{2,1,0:T(8,128)(2,1)}, u32[]{:S(2)}) copy-start(bf16[2,128,2048]{2,1,0:T(8,128)(2,1)} %param.5) | copy-start | bytes 3145732
Sparse Core Ops, SparseCore 0:
  75.1 54.2 all-gather.1
where the time goes:
time: 215 us; the launch traced here: 214 us
  blocking collectives  58.8 us (27%)
  waiting for transfers between devices  53.1 us (25%)
  matrix products  51.3 us (24%)
  local copies, waits for them, and re-layouts  27.8 us (13%)
  between operations  13.5 us (6%)
  other arithmetic  9.15 us (4%)
    all_gather x1, waiting for transfers between devices, per_device(): kv_all = lax.all_gather(qkv_grp[:, :, 1:], 'row', axis=1, tiled=True)  53 us
    all_to_all x1, blocking collectives, per_device(): qkv_grp = lax.all_to_all(qkv_loc, head_axes, 3, 1, tiled=True)  41.3 us
    dot_general x8, matrix products, key_step(): jnp.einsum('bhqk,bkhd->bhqd', weights.astype(jnp.bfloat16), kv_piece[:, :...  18.9 us
    all_to_all x1, blocking collectives, per_device(): attn_loc = lax.all_to_all(attn_out, head_axes, 1, 2, tiled=True)  17.5 us
    dot_general x8, matrix products, key_step(): jnp.einsum('bqhd,bkhd->bhqk', queries, kv_piece[:, :, 0], preferred_eleme...  13.8 us
    dot_general x1, matrix products, per_device(): jnp.einsum('btc,cjhd->btjhd', tokens, w_qkv, preferred_element_type=jnp.f...  11.6 us
    all_to_all x2, local copies, waits for them, and re-layouts, per_device(): qkv_grp = lax.all_to_all(qkv_loc, head_axes, 3, 1, tiled=True)  10.4 us
    dot_general x1, matrix products, per_device(): jnp.einsum('bthd,hdc->btc', attn_loc, w_out, preferred_element_type=jnp.f...  7.1 us
  transfers between devices with their start and end apart: 1, of which 1 were waited for; matrix products, arithmetic and copies ran while one was open for 1% of the time, Pallas kernels for 0%

commit v1 on v0

v1 whole, which is shorter than its diff:
```python
import functools

import jax
import jax.numpy as jnp
from jax import lax
from jax.experimental import pallas as pl
from jax.experimental.pallas import tpu as pltpu
from jax.sharding import PartitionSpec as P

BF = jnp.bfloat16
F32 = jnp.float32
NN = (((1,), (0,)), ((), ()))
NT = (((1,), (1,)), ((), ()))
MESH = pl.DeviceIdType.MESH
LOG2E = 1.4426950408889634
BLOCKS = 8
HALF = 1024
PAIRS = 8
STEPS = 16


def dot(a, b, dims):
    return lax.dot_general(a, b, dims, preferred_element_type=F32)


def kernel(
    x_hbm, wt_hbm, wo_hbm, y_ref,
    xbuf, wq, wk, wv, wo, qz, kbuf, vbuf, acc, m_ref, l_ref, s0, s1, p0, p1, a0, a1, o_own, o_out, o_in, y_acc,
    w_sem, xl_sem, own_send, own_recv, ici_send, ici_recv, rel_send, rel_recv, o_sem,
):
    row, col, core = lax.axis_index("row"), lax.axis_index("col"), lax.axis_index("core")
    x_nbr, y_nbr, mate = {"col": 1 - col}, {"row": 1 - row}, {"core": 1 - core}

    def w_copy(j, i, dst):
        start = pl.multiple_of(j * 2048 + core * HALF + i * 256, 256)
        return pltpu.make_async_copy(wt_hbm.at[pl.ds(start, 256)], dst.at[pl.ds(i * 256, 256)], w_sem.at[j * 4 + i])

    w_copies = [w_copy(j, i, dst) for j, dst in enumerate((wq, wk, wv)) for i in range(4)]
    wo_copy = pltpu.make_async_copy(wo_hbm, wo, w_sem.at[12])
    x_local = pltpu.make_async_copy(x_hbm, xbuf.at[0], xl_sem)
    x_local.start()
    for c in w_copies:
        c.start()

    barrier = pltpu.get_barrier_semaphore()
    for dev in (x_nbr, y_nbr, mate):
        pl.semaphore_signal(barrier, inc=1, device_id=dev, device_id_type=MESH)
    pl.semaphore_wait(barrier, 3)

    def remote(src, dst, send, recv, dev):
        return pltpu.make_async_remote_copy(
            src_ref=src, dst_ref=dst, send_sem=send, recv_sem=recv, device_id=dev, device_id_type=MESH
        )

    to_mate = remote(x_hbm, xbuf.at[1], own_send, own_recv, mate)
    to_mate.start()

    def ici(b, s):
        first = b < 4
        dev = x_nbr if first == (s == 0) else y_nbr
        return remote(
            x_hbm.at[pl.ds(s * 128 + (b % 2) * 64, 64)], xbuf.at[b, pl.ds(s * 128, 64)],
            ici_send.at[b, s], ici_recv.at[b, s], dev,
        )

    sends = [ici(b, s) for b in range(2, 6) for s in range(2)]
    for c in sends:
        c.start()

    def forward(b, s):
        return remote(
            xbuf.at[b, pl.ds(s * 128, 64)], xbuf.at[b + 4, pl.ds(s * 128, 64)],
            ici_send.at[b + 4, s], ici_recv.at[b + 4, s], y_nbr if s == 0 else x_nbr,
        )

    def relay(b, s):
        return remote(
            xbuf.at[b, pl.ds(s * 128, 64)], xbuf.at[b, pl.ds(s * 128 + 64, 64)],
            rel_send.at[b, s], rel_recv.at[b, s], mate,
        )

    def arrived(b, s):
        piece = xbuf.at[b, pl.ds(s * 128, 64)]
        return remote(piece, piece, ici_send.at[b, s], ici_recv.at[b, s], mate)

    qz[...] = jnp.zeros_like(qz)
    acc[...] = jnp.zeros_like(acc)
    l_ref[...] = jnp.zeros_like(l_ref)
    m_ref[...] = jnp.full_like(m_ref, -jnp.inf)

    def query_tile(blk, i):
        q_t = (dot(wq[pl.ds(i * 256, 256), :], xbuf[blk], NT) * 0.125).astype(BF)
        for pair in range(2):
            for s in range(2):
                for h in range(2):
                    piece = q_t[pair * 128 + h * 64 : pair * 128 + h * 64 + 64, s * 128 : s * 128 + 128]
                    lanes = h * 256 + blk * 128
                    qz[(i * 2 + pair) * 2 + s, h * 64 : h * 64 + 64, lanes : lanes + 128] = piece

    x_local.wait()
    for i in range(4):
        w_copies[i].wait()
        query_tile(0, i)
    to_mate.wait_recv()
    for i in range(4):
        query_tile(1, i)
    wo_copy.start()
    for c in w_copies[4:]:
        c.wait()

    def scores(t, s_out):
        s, j = t % 2, t // 2
        keys = kbuf[s * 128 : s * 128 + 128, j * 128 : j * 128 + 128]
        s_out[...] = dot(keys, qz[t], NN)

    def weigh(t, s_in, p_out, a_out):
        sc = s_in[...]
        old = m_ref[t]
        new = jnp.maximum(old, jnp.max(sc, axis=0, keepdims=True))
        p = jnp.exp2((sc - new) * LOG2E)
        scale = jnp.exp2((old - new) * LOG2E)
        l_ref[t] = l_ref[t] * scale + jnp.sum(p, axis=0, keepdims=True)
        m_ref[t] = new
        p_out[...] = p.astype(BF)
        a_out[...] = scale

    def add_values(t, p_in, a_in):
        s, j = t % 2, t // 2
        for h in range(2):
            vals = vbuf[j * 128 + h * 64 : j * 128 + h * 64 + 64, s * 128 : s * 128 + 128]
            lanes = slice(h * 256, h * 256 + 256)
            acc[2 * t + h] = acc[2 * t + h] * a_in[:, lanes] + dot(vals, p_in[:, lanes], NN)

    s_b, p_b, a_b = (s0, s1), (p0, p1), (a0, a1)

    def block(b, carry):
        @pl.when(b >= 2)
        def _():
            for s in range(2):
                relay(b, s).wait_recv()

        for n in range(2):
            kbuf[:, n * 512 : n * 512 + 512] = dot(xbuf[b], wk[n * 512 : n * 512 + 512, :], NT).astype(BF)
        for n in range(2):
            vbuf[n * 512 : n * 512 + 512, :] = dot(wv[n * 512 : n * 512 + 512, :], xbuf[b], NT).astype(BF)

        @pl.when((b >= 1) & (b < BLOCKS - 1))
        def _():
            for s in range(2):
                arrived(b + 1, s).wait_recv()
                relay(b + 1, s).start()

        @pl.when((b >= 1) & (b < 3))
        def _():
            for s in range(2):
                forward(b + 1, s).start()

        scores(0, s0)
        scores(1, s1)
        weigh(0, s0, p0, a0)
        for t in range(STEPS):
            if t + 2 < STEPS:
                scores(t + 2, s_b[t % 2])
            if t + 1 < STEPS:
                weigh(t + 1, s_b[(t + 1) % 2], p_b[(t + 1) % 2], a_b[(t + 1) % 2])
            add_values(t, p_b[t % 2], a_b[t % 2])
        return carry

    lax.fori_loop(0, BLOCKS, block, 0)

    for s in range(2):
        for j in range(PAIRS):
            t = 2 * j + s
            parts = [acc[2 * t + h] / l_ref[t][:, h * 256 : h * 256 + 256] for h in range(2)]
            o_rows = jnp.concatenate(parts, axis=0).T.astype(BF)
            o_own[s * 128 : s * 128 + 128, j * 128 : j * 128 + 128] = o_rows[:128]
            o_out[s * 128 : s * 128 + 128, j * 128 : j * 128 + 128] = o_rows[128:]
    o_copy = remote(o_out, o_in, o_sem.at[0], o_sem.at[1], mate)
    o_copy.start()
    wo_copy.wait()
    mine = pl.multiple_of(core * HALF, HALF)
    theirs = pl.multiple_of((1 - core) * HALF, HALF)
    for n in range(4):
        y_acc[:, n * 512 : n * 512 + 512] = dot(o_own[...], wo[pl.ds(mine, HALF), n * 512 : n * 512 + 512], NN)
    o_copy.wait()
    for n in range(4):
        more = dot(o_in[...], wo[pl.ds(theirs, HALF), n * 512 : n * 512 + 512], NN)
        y_ref[:, n * 512 : n * 512 + 512] = (y_acc[:, n * 512 : n * 512 + 512] + more).astype(BF)

    to_mate.wait_send()
    for c in sends:
        c.wait_send()
    for b in range(2, 4):
        for s in range(2):
            forward(b, s).wait_send()
    for b in range(2, BLOCKS):
        for s in range(2):
            relay(b, s).wait_send()


def solution(mesh):
    tok_spec = P("data", ("row", "col", "core"), None)

    def per_device(tokens, w_qkv, w_out):
        x = tokens.reshape(256, 2048)
        wt = jnp.transpose(w_qkv, (1, 2, 3, 0)).reshape(6144, 2048)
        wo = w_out.reshape(2048, 2048)
        dma = pltpu.SemaphoreType.DMA
        y = pl.pallas_call(
            kernel,
            out_shape=jax.ShapeDtypeStruct((256, 2048), BF),
            in_specs=[pl.BlockSpec(memory_space=pl.ANY)] * 3,
            out_specs=pl.BlockSpec(memory_space=pltpu.VMEM),
            scratch_shapes=[
                pltpu.VMEM((BLOCKS, 256, 2048), BF),
                pltpu.VMEM((HALF, 2048), BF),
                pltpu.VMEM((HALF, 2048), BF),
                pltpu.VMEM((HALF, 2048), BF),
                pltpu.VMEM((2048, 2048), BF),
                pltpu.VMEM((STEPS, 128, 512), BF),
                pltpu.VMEM((256, HALF), BF),
                pltpu.VMEM((HALF, 256), BF),
                pltpu.VMEM((2 * STEPS, 64, 256), F32),
                pltpu.VMEM((STEPS, 1, 512), F32),
                pltpu.VMEM((STEPS, 1, 512), F32),
                pltpu.VMEM((128, 512), F32),
                pltpu.VMEM((128, 512), F32),
                pltpu.VMEM((128, 512), BF),
                pltpu.VMEM((128, 512), BF),
                pltpu.VMEM((1, 512), F32),
                pltpu.VMEM((1, 512), F32),
                pltpu.VMEM((256, HALF), BF),
                pltpu.VMEM((256, HALF), BF),
                pltpu.VMEM((256, HALF), BF),
                pltpu.VMEM((256, 2048), F32),
                dma((13,)),
                dma,
                dma,
                dma,
                dma((BLOCKS, 2)),
                dma((BLOCKS, 2)),
                dma((BLOCKS, 2)),
                dma((BLOCKS, 2)),
                dma((2,)),
            ],
            compiler_params=pltpu.CompilerParams(
                collective_id=0, has_side_effects=True, vmem_limit_bytes=58 * 1024 * 1024
            ),
            name="attention",
        )(x, wt, wo)
        return y.reshape(2, 128, 2048)

    return jax.shard_map(per_device, mesh=mesh, in_specs=(tok_spec, P(), P()), out_specs=tok_spec, check_vma=False)
```

time: 215 us -> 52.2 us (0.24)
  blocking collectives: 58.8 us -> 0 us
  waiting for transfers between devices: 53.1 us -> 0 us
  matrix products: 51.3 us -> 0 us
  Pallas kernels: 0 us -> 49.8 us
  local copies, waits for them, and re-layouts: 27.8 us -> 2.3 us
  between operations: 13.5 us -> 0.01 us
  other arithmetic: 9.15 us -> 0 us
    all_to_all x2 -> x0, blocking collectives: 58.8 us -> none  [the longest x1 41.3 us: per_device(): qkv_grp = lax.all_to_all(qkv_loc, head_axes, 3, 1, tiled=True)]
    all_gather x1 -> x0, waiting for transfers between devices: 53 us -> none  [per_device(): kv_all = lax.all_gather(qkv_grp[:, :, 1:], 'row', axis=1, tiled=True)]
    dot_general x18 -> x0, matrix products: 51.3 us -> none  [the longest x8 18.9 us: key_step(): jnp.einsum('bhqk,bkhd->bhqd', weights.astype(jnp.bfloat16), kv_piece[:, :...]
    pallas_call x0 -> x1, Pallas kernels: none -> 49.8 us  [per_device(): pl.pallas_call(kernel, out_shape=jax.ShapeDtypeStruct((256, 2048), BF), i...]
    all_to_all x3 -> x0, local copies, waits for them, and re-layouts: 12.5 us -> none  [the longest x2 10.4 us: per_device(): qkv_grp = lax.all_to_all(qkv_loc, head_axes, 3, 1, tiled=True)]
    reduce_sum x8 -> x0, other arithmetic: 6.06 us -> none  [key_step(): run_sum = run_sum * rescale + jnp.sum(weights, axis=-1)]
    while x10 -> x0, local copies, waits for them, and re-layouts: 4.04 us -> none  [the longest x2 4.01 us: attend_keys(): return lax.fori_loop(0, kv_rows.shape[1] // blk_len, key_step, state)]
    unnamed x6 -> x1, local copies, waits for them, and re-layouts: 5.98 us -> 2.3 us
  transfers between devices with their start and end apart: 1 -> 0, of which waited for: 1 -> 0; matrix products, arithmetic and copies ran while one was open for 1% -> 0% of each run, Pallas kernels for 0% -> 0%
where the time goes in v1:
time: 52.2 us; the launch traced here: 52.1 us
  Pallas kernels  49.8 us (95%)
  local copies, waits for them, and re-layouts  2.3 us (4%)
    pallas_call x1, Pallas kernels, per_device(): pl.pallas_call(kernel, out_shape=jax.ShapeDtypeStruct((256, 2048), BF), i...  49.8 us
    unnamed x1, local copies, waits for them, and re-layouts  2.3 us

profile of v1, /device:TPU:0, one launch (start us, length us, event | category | flops | bytes accessed | tf_op | source)
XLA Modules:
  0.0 52.1 jit_solution(12617149102234129509)
XLA Ops:
  0.0 49.8 %attention.1 = bf16[256,2048]{1,0:T(8,128)(2,1)} custom-call(bf16[256,2048]{1,0:T(8,128)(2,1)} %bitcast.9, bf16[6144,2048]{1,0:T(8,128)(2,1)} %bitcast.6, bf16[2048,2048]{1,0:T(8,128)(2,1)} %bitcast.7), custom_call_target="tpu_custom_call" | custom-call | tf_op jit(solution)/shard_map/attention/pallas_call | solution.py:209
  49.8 2.3 %copy.5 = bf16[2,128,2048]{2,1,0:T(8,128)(2,1)} copy(bf16[2,128,2048]{2,1,0:T(8,128)(2,1)} %bitcast.8) | data formatting | bytes 2097152

commit v2 on v1

v2 whole, which is shorter than its diff:
```python
import functools

import jax
import jax.numpy as jnp
from jax import lax
from jax.experimental import pallas as pl
from jax.experimental.pallas import tpu as pltpu
from jax.sharding import PartitionSpec as P

BF = jnp.bfloat16
F32 = jnp.float32
NN = (((1,), (0,)), ((), ()))
NT = (((1,), (1,)), ((), ()))
MESH = pl.DeviceIdType.MESH
LOG2E = 1.4426950408889634
BLOCKS = 8
HALF = 1024
PAIRS = 8
STEPS = 16
AHEAD = 3
LAG = 1
FIRST_PART = 5
PARTS = 2
WIDE = 2048 // PARTS


def dot(a, b, dims):
    return lax.dot_general(a, b, dims, preferred_element_type=F32)


def kernel(
    x_hbm, wt_hbm, wo_hbm, y_ref,
    xbuf, wq, wk, wv, wo, k_acc, v_acc, acc, m_ref, l_ref, o_buf, o_out,
    w_sem, xl_sem, own_send, own_recv, ici_send, ici_recv, rel_send, rel_recv,
    part_send, part_recv, prel_send, prel_recv, o_send, o_recv,
    qz, kbuf, vbuf, *bufs,
):
    s_b, p_b, a_b = bufs[:AHEAD], bufs[AHEAD : AHEAD + LAG + 1], bufs[AHEAD + LAG + 1 :]
    row, col, core = lax.axis_index("row"), lax.axis_index("col"), lax.axis_index("core")
    x_nbr, y_nbr, mate = {"col": 1 - col}, {"row": 1 - row}, {"core": 1 - core}
    mine = pl.multiple_of(core * HALF, HALF)
    theirs = pl.multiple_of((1 - core) * HALF, HALF)

    def w_copy(j, i, dst):
        start = pl.multiple_of(j * 2048 + core * HALF + i * 256, 256)
        return pltpu.make_async_copy(wt_hbm.at[pl.ds(start, 256)], dst.at[pl.ds(i * 256, 256)], w_sem.at[j * 4 + i])

    wq_copies, wk_copies, wv_copies = [[w_copy(j, i, dst) for i in range(4)] for j, dst in enumerate((wq, wk, wv))]
    wo_copies = [
        pltpu.make_async_copy(wo_hbm.at[pl.ds(start, HALF)], wo.at[pl.ds(i * HALF, HALF)], w_sem.at[12 + i])
        for i, start in enumerate((mine, theirs))
    ]
    x_locals = [
        pltpu.make_async_copy(x_hbm.at[pl.ds(i * 64, 64)], xbuf.at[0, pl.ds(i * 64, 64)], xl_sem.at[i])
        for i in range(4)
    ]
    for c in x_locals:
        c.start()
    barrier = pltpu.get_barrier_semaphore()
    for dev in (x_nbr, y_nbr, mate):
        pl.semaphore_signal(barrier, inc=1, device_id=dev, device_id_type=MESH)
    qz[...] = jnp.zeros_like(qz)
    acc[...] = jnp.zeros_like(acc)
    l_ref[...] = jnp.zeros_like(l_ref)
    m_ref[...] = jnp.full_like(m_ref, -jnp.inf)
    for c in x_locals:
        c.wait()
    for c in wq_copies:
        c.start()
    pl.semaphore_wait(barrier, 3)

    def remote(src, dst, send, recv, dev):
        return pltpu.make_async_remote_copy(
            src_ref=src, dst_ref=dst, send_sem=send, recv_sem=recv, device_id=dev, device_id_type=MESH
        )

    def piece(b, s, second=False):
        return xbuf.at[b, pl.ds(s * 128 + (64 if second else 0), 64)]

    def part(b, s, c, second=False):
        return xbuf.at[b, pl.ds(s * 128 + (64 if second else 0), 64), pl.ds(c * WIDE, WIDE)]

    def link_of(b, s):
        return x_nbr if (b < 4) == (s == 0) else y_nbr

    def direct(b, s):
        src = xbuf.at[0, pl.ds(s * 128 + (b % 2) * 64, 64)]
        return remote(src, piece(b, s), ici_send.at[b, s], ici_recv.at[b, s], link_of(b, s))

    def direct_part(b, s, c):
        src = xbuf.at[0, pl.ds(s * 128 + (b % 2) * 64, 64), pl.ds(c * WIDE, WIDE)]
        i = b - FIRST_PART
        return remote(src, part(b, s, c), part_send.at[i, s, c], part_recv.at[i, s, c], link_of(b, s))

    def forward_part(b, s, c):
        i = b + 4 - FIRST_PART
        dev = y_nbr if s == 0 else x_nbr
        return remote(part(b, s, c), part(b + 4, s, c), part_send.at[i, s, c], part_recv.at[i, s, c], dev)

    def relay(b, s):
        return remote(piece(b, s), piece(b, s, True), rel_send.at[b, s], rel_recv.at[b, s], mate)

    def relay_part(b, s, c):
        i = b - FIRST_PART
        return remote(part(b, s, c), part(b, s, c, True), prel_send.at[i, s, c], prel_recv.at[i, s, c], mate)

    def arrived(b, s):
        return remote(piece(b, s), piece(b, s), ici_send.at[b, s], ici_recv.at[b, s], mate)

    def arrived_part(b, s, c):
        i = b - FIRST_PART
        return remote(part(b, s, c), part(b, s, c), part_send.at[i, s, c], part_recv.at[i, s, c], mate)

    to_mate = remote(xbuf.at[0], xbuf.at[1], own_send, own_recv, mate)
    sends = []
    for b, s in ((2, 0), (2, 1), (3, 0), (3, 1), (4, 0), (4, 1), (5, 0), (5, 1)):
        if b == 4 and s == 0:
            to_mate.start()
        if b < FIRST_PART:
            sends.append(direct(b, s))
            sends[-1].start()
        for c in range(PARTS if b >= FIRST_PART else 0):
            sends.append(direct_part(b, s, c))
            sends[-1].start()

    def query_tile(blk, i):
        q_t = (dot(wq[pl.ds(i * 256, 256), :], xbuf[blk], NT) * 0.125).astype(BF)
        for pair in range(2):
            for s in range(2):
                for h in range(2):
                    tile = q_t[pair * 128 + h * 64 : pair * 128 + h * 64 + 64, s * 128 : s * 128 + 128]
                    lanes = h * 256 + blk * 128
                    qz[(i * 2 + pair) * 2 + s, h * 64 : h * 64 + 64, lanes : lanes + 128] = tile

    for i in range(4):
        wq_copies[i].wait()
        for c in (wk_copies + wv_copies)[2 * i : 2 * i + 2]:
            c.start()
        query_tile(0, i)
    to_mate.wait_recv()
    for i in range(4):
        query_tile(1, i)
    for c in wk_copies + wv_copies:
        c.wait()
    for c in wo_copies:
        c.start()

    def scores(t, s_out):
        s, j = t % 2, t // 2
        s_out[...] = dot(kbuf[s * 128 : s * 128 + 128, j * 128 : j * 128 + 128], qz[t], NN)

    def weigh(t, s_in, p_out, a_out):
        sc = s_in[...]
        old = m_ref[t]
        new = jnp.maximum(old, jnp.max(sc, axis=0, keepdims=True))
        p = jnp.exp2((sc - new) * LOG2E)
        scale = jnp.exp2((old - new) * LOG2E)
        l_ref[t] = l_ref[t] * scale + jnp.sum(p.reshape(16, 8, 512), axis=0)
        m_ref[t] = new
        p_out[...] = p.astype(BF)
        a_out[...] = scale

    def add_values(t, p_in, a_in):
        s, j = t % 2, t // 2
        for h in range(2):
            vals = vbuf[j * 128 + h * 64 : j * 128 + h * 64 + 64, s * 128 : s * 128 + 128]
            lanes = slice(h * 256, h * 256 + 256)
            acc[2 * t + h] = acc[2 * t + h] * a_in[:, lanes] + dot(vals, p_in[:, lanes], NN)

    def attend(order, hooks):
        def weigh_step(i):
            weigh(order[i], s_b[i % AHEAD], p_b[i % (LAG + 1)], a_b[i % (LAG + 1)])

        for i in range(AHEAD):
            scores(order[i], s_b[i])
        for i in range(LAG):
            weigh_step(i)
        for i, t in enumerate(order):
            if i + LAG < STEPS:
                weigh_step(i + LAG)
            if i + AHEAD < STEPS:
                scores(order[i + AHEAD], s_b[i % AHEAD])
            add_values(t, p_b[i % (LAG + 1)], a_b[i % (LAG + 1)])
            if i in hooks:
                hooks[i]()

    def pass_on(b, c):
        for s in range(2):
            arrived_part(b, s, c).wait_recv()
            relay_part(b, s, c).start()

    def block(b, carry):
        @pl.when(b >= 2)
        def _():
            for s in range(2):
                relay(b, s).wait_recv()

        for n in range(2):
            kbuf[:, n * 512 : n * 512 + 512] = dot(xbuf[b], wk[n * 512 : n * 512 + 512, :], NT).astype(BF)
        for n in range(2):
            vbuf[n * 512 : n * 512 + 512, :] = dot(wv[n * 512 : n * 512 + 512, :], xbuf[b], NT).astype(BF)

        @pl.when((b >= 1) & (b < FIRST_PART - 1))
        def _():
            for s in range(2):
                arrived(b + 1, s).wait_recv()
                relay(b + 1, s).start()

        @pl.when((b >= 1) & (b < 3))
        def _():
            for c in range(PARTS):
                for s in range(2):
                    forward_part(b + 1, s, c).start()

        @pl.when(b == FIRST_PART - 1)
        def _():
            pass_on(FIRST_PART, 0)

        attend(list(range(STEPS)), {})
        return carry

    lax.fori_loop(0, FIRST_PART, block, 0)

    def project_part(b, c):
        cols = slice(c * WIDE, c * WIDE + WIDE)
        x_part = xbuf[b, :, cols]
        for n in range(2):
            lanes = slice(n * 512, n * 512 + 512)
            k_new = dot(x_part, wk[lanes, cols], NT)
            v_new = dot(wv[lanes, cols], x_part, NT)
            if c > 0:
                k_new += k_acc[:, lanes]
                v_new += v_acc[lanes, :]
            if c < PARTS - 1:
                k_acc[:, lanes] = k_new
                v_acc[lanes, :] = v_new
            else:
                kbuf[:, lanes] = k_new.astype(BF)
                vbuf[lanes, :] = v_new.astype(BF)

    def project_parts(b):
        for c in range(PARTS):
            if c + 1 < PARTS:
                pass_on(b, c + 1)
            for s in range(2):
                relay_part(b, s, c).wait_recv()
            project_part(b, c)

    for b in range(FIRST_PART, BLOCKS):
        project_parts(b)
        if b < BLOCKS - 1:
            pass_on(b + 1, 0)
            attend(list(range(STEPS)), {})

    def o_copy(s):
        dst = o_buf.at[pl.ds(s * 128, 128), pl.ds(HALF, HALF)]
        return remote(o_out.at[pl.ds(s * 128, 128)], dst, o_send.at[s], o_recv.at[s], mate)

    def finish(s):
        for j in range(PAIRS):
            t = 2 * j + s
            total = jnp.sum(l_ref[t], axis=0, keepdims=True)
            parts = [acc[2 * t + h] / total[:, h * 256 : h * 256 + 256] for h in range(2)]
            o_rows = jnp.concatenate(parts, axis=0).T.astype(BF)
            o_out[s * 128 : s * 128 + 128, j * 128 : j * 128 + 128] = o_rows[128:]
            o_buf[s * 128 : s * 128 + 128, j * 128 : j * 128 + 128] = o_rows[:128]
        o_copy(s).start()

    attend([2 * j + s for s in range(2) for j in range(PAIRS)], {STEPS // 2 - 1: lambda: finish(0)})
    finish(1)
    for c in wo_copies:
        c.wait()
    for s in range(2):
        o_copy(s).wait_recv()
        for n in range(4):
            lanes = slice(n * 512, n * 512 + 512)
            y_ref[s * 128 : s * 128 + 128, lanes] = dot(o_buf[s * 128 : s * 128 + 128, :], wo[:, lanes], NN).astype(BF)

    to_mate.wait_send()
    for c in sends:
        c.wait_send()
    for s in range(2):
        o_copy(s).wait_send()
        for b in range(2, FIRST_PART):
            relay(b, s).wait_send()
        for c in range(PARTS):
            for b in range(2, 4):
                forward_part(b, s, c).wait_send()
            for b in range(FIRST_PART, BLOCKS):
                relay_part(b, s, c).wait_send()


def solution(mesh):
    tok_spec = P("data", ("row", "col", "core"), None)

    def per_device(tokens, w_qkv, w_out):
        x = tokens.reshape(256, 2048)
        wt = jnp.transpose(w_qkv, (1, 2, 3, 0)).reshape(6144, 2048)
        wo = w_out.reshape(2048, 2048)
        dma = pltpu.SemaphoreType.DMA
        local = [
            pltpu.VMEM((STEPS, 128, 512), BF),
            pltpu.VMEM((256, HALF), BF),
            pltpu.VMEM((HALF, 256), BF),
            *[pltpu.VMEM((128, 512), F32)] * AHEAD,
            *[pltpu.VMEM((128, 512), BF)] * (LAG + 1),
            *[pltpu.VMEM((1, 512), F32)] * (LAG + 1),
        ]
        y = pl.pallas_call(
            lambda *refs: pl.run_scoped(functools.partial(kernel, *refs), *local),
            out_shape=jax.ShapeDtypeStruct((256, 2048), BF),
            in_specs=[pl.BlockSpec(memory_space=pl.ANY)] * 3,
            out_specs=pl.BlockSpec(memory_space=pltpu.VMEM),
            scratch_shapes=[
                pltpu.VMEM((BLOCKS, 256, 2048), BF),
                pltpu.VMEM((HALF, 2048), BF),
                pltpu.VMEM((HALF, 2048), BF),
                pltpu.VMEM((HALF, 2048), BF),
                pltpu.VMEM((2048, 2048), BF),
                pltpu.VMEM((256, HALF), F32),
                pltpu.VMEM((HALF, 256), F32),
                pltpu.VMEM((2 * STEPS, 64, 256), F32),
                pltpu.VMEM((STEPS, 1, 512), F32),
                pltpu.VMEM((STEPS, 8, 512), F32),
                pltpu.VMEM((256, 2048), BF),
                pltpu.VMEM((256, HALF), BF),
                dma((14,)),
                dma((4,)),
                dma,
                dma,
                dma((FIRST_PART, 2)),
                dma((FIRST_PART, 2)),
                dma((FIRST_PART, 2)),
                dma((FIRST_PART, 2)),
                dma((BLOCKS - FIRST_PART, 2, PARTS)),
                dma((BLOCKS - FIRST_PART, 2, PARTS)),
                dma((BLOCKS - FIRST_PART, 2, PARTS)),
                dma((BLOCKS - FIRST_PART, 2, PARTS)),
                dma((2,)),
                dma((2,)),
            ],
            compiler_params=pltpu.CompilerParams(
                collective_id=0, has_side_effects=True, vmem_limit_bytes=52 * 1024 * 1024
            ),
            name="attention",
        )(x, wt, wo)
        return y.reshape(2, 128, 2048)

    return jax.shard_map(per_device, mesh=mesh, in_specs=(tok_spec, P(), P()), out_specs=tok_spec, check_vma=False)
```

time: 52.2 us -> 48.6 us (0.931)
  Pallas kernels: 49.8 us -> 47.5 us
  local copies, waits for them, and re-layouts: 2.3 us -> 0.97 us
    pallas_call x1, Pallas kernels: 49.8 us -> 47.5 us  [per_device(): pl.pallas_call(lambda *refs: pl.run_scoped(functools.partial(kernel, *ref...]
    unnamed x1, local copies, waits for them, and re-layouts: 2.3 us -> 0.97 us
where the time goes in v2:
time: 48.6 us; the launch traced here: 48.5 us
  Pallas kernels  47.5 us (98%)
  local copies, waits for them, and re-layouts  0.97 us (2%)
    pallas_call x1, Pallas kernels, per_device(): pl.pallas_call(lambda *refs: pl.run_scoped(functools.partial(kernel, *ref...  47.5 us
    unnamed x1, local copies, waits for them, and re-layouts  0.97 us

profile of v2, /device:TPU:0, one launch (start us, length us, event | category | flops | bytes accessed | tf_op | source)
XLA Modules:
  0.0 48.5 jit_solution(17413281698191532090)
XLA Ops:
  0.0 47.5 %attention.1 = bf16[256,2048]{1,0:T(8,128)(2,1)S(1)} custom-call(bf16[256,2048]{1,0:T(8,128)(2,1)} %bitcast.9, bf16[6144,2048]{1,0:T(8,128)(2,1)} %bitcast.7, bf16[2048,2048]{1,0:T(8,128)(2,1)} %bitcast.8), custom_call_target="tpu_custom_call" | custom-call | tf_op jit(solution)/shard_map/attention/pallas_call | solution.py:309
  47.5 1.0 %copy.5 = bf16[2,128,2048]{2,1,0:T(8,128)(2,1)} copy(bf16[2,128,2048]{2,1,0:T(8,128)(2,1)S(1)} %bitcast.6) | data formatting | bytes 2097152

commit v3 on v2

--- a/solution.py
+++ b/solution.py
@@ -19,9 +19,9 @@
 STEPS = 16
 AHEAD = 3
 LAG = 1
-FIRST_PART = 5
-PARTS = 2
-WIDE = 2048 // PARTS
+FIRST_PART = 6
+COLS = (0, 1024, 2048)
+PARTS = len(COLS) - 1
 
 
 def dot(a, b, dims):
@@ -30,7 +30,7 @@
 
 def kernel(
     x_hbm, wt_hbm, wo_hbm, y_ref,
-    xbuf, wq, wk, wv, wo, k_acc, v_acc, acc, m_ref, l_ref, o_buf, o_out,
+    xbuf, wq, wk, wv, wo, k_acc, v_acc, acc, m_ref, l_ref, o_buf, o_out, y_acc,
     w_sem, xl_sem, own_send, own_recv, ici_send, ici_recv, rel_send, rel_recv,
     part_send, part_recv, prel_send, prel_recv, o_send, o_recv,
     qz, kbuf, vbuf, *bufs,
@@ -78,7 +78,7 @@
         return xbuf.at[b, pl.ds(s * 128 + (64 if second else 0), 64)]
 
     def part(b, s, c, second=False):
-        return xbuf.at[b, pl.ds(s * 128 + (64 if second else 0), 64), pl.ds(c * WIDE, WIDE)]
+        return xbuf.at[b, pl.ds(s * 128 + (64 if second else 0), 64), pl.ds(COLS[c], COLS[c + 1] - COLS[c])]
 
     def link_of(b, s):
         return x_nbr if (b < 4) == (s == 0) else y_nbr
@@ -88,7 +88,7 @@
         return remote(src, piece(b, s), ici_send.at[b, s], ici_recv.at[b, s], link_of(b, s))
 
     def direct_part(b, s, c):
-        src = xbuf.at[0, pl.ds(s * 128 + (b % 2) * 64, 64), pl.ds(c * WIDE, WIDE)]
+        src = xbuf.at[0, pl.ds(s * 128 + (b % 2) * 64, 64), pl.ds(COLS[c], COLS[c + 1] - COLS[c])]
         i = b - FIRST_PART
         return remote(src, part(b, s, c), part_send.at[i, s, c], part_recv.at[i, s, c], link_of(b, s))
 
@@ -189,7 +189,7 @@
             arrived_part(b, s, c).wait_recv()
             relay_part(b, s, c).start()
 
-    def block(b, carry):
+    def whole_block(b):
         @pl.when(b >= 2)
         def _():
             for s in range(2):
@@ -216,13 +216,8 @@
         def _():
             pass_on(FIRST_PART, 0)
 
-        attend(list(range(STEPS)), {})
-        return carry
-
-    lax.fori_loop(0, FIRST_PART, block, 0)
-
     def project_part(b, c):
-        cols = slice(c * WIDE, c * WIDE + WIDE)
+        cols = slice(COLS[c], COLS[c + 1])
         x_part = xbuf[b, :, cols]
         for n in range(2):
             lanes = slice(n * 512, n * 512 + 512)
@@ -238,7 +233,7 @@
                 kbuf[:, lanes] = k_new.astype(BF)
                 vbuf[lanes, :] = v_new.astype(BF)
 
-    def project_parts(b):
+    def part_block(b):
         for c in range(PARTS):
             if c + 1 < PARTS:
                 pass_on(b, c + 1)
@@ -246,11 +241,21 @@
                 relay_part(b, s, c).wait_recv()
             project_part(b, c)
 
-    for b in range(FIRST_PART, BLOCKS):
-        project_parts(b)
-        if b < BLOCKS - 1:
+    def block(b, carry):
+        @pl.when(b < FIRST_PART)
+        def _():
+            whole_block(b)
+
+        @pl.when(b >= FIRST_PART)
+        def _():
+            part_block(b)
             pass_on(b + 1, 0)
-            attend(list(range(STEPS)), {})
+
+        attend(list(range(STEPS)), {})
+        return carry
+
+    lax.fori_loop(0, BLOCKS - 1, block, 0)
+    part_block(BLOCKS - 1)
 
     def o_copy(s):
         dst = o_buf.at[pl.ds(s * 128, 128), pl.ds(HALF, HALF)]
@@ -266,15 +271,30 @@
             o_buf[s * 128 : s * 128 + 128, j * 128 : j * 128 + 128] = o_rows[:128]
         o_copy(s).start()
 
-    attend([2 * j + s for s in range(2) for j in range(PAIRS)], {STEPS // 2 - 1: lambda: finish(0)})
-    finish(1)
     for c in wo_copies:
         c.wait()
-    for s in range(2):
-        o_copy(s).wait_recv()
-        for n in range(4):
-            lanes = slice(n * 512, n * 512 + 512)
-            y_ref[s * 128 : s * 128 + 128, lanes] = dot(o_buf[s * 128 : s * 128 + 128, :], wo[:, lanes], NN).astype(BF)
+
+    def own_share(s, n):
+        rows, lanes = slice(s * 128, s * 128 + 128), slice(n * 512, n * 512 + 512)
+        y_acc[rows, lanes] = dot(o_buf[rows, :HALF], wo[:HALF, lanes], NN)
+
+    def other_share(s, n):
+        rows, lanes = slice(s * 128, s * 128 + 128), slice(n * 512, n * 512 + 512)
+        y_ref[rows, lanes] = (y_acc[rows, lanes] + dot(o_buf[rows, HALF:], wo[HALF:, lanes], NN)).astype(BF)
+
+    hooks = {PAIRS - 1: lambda: finish(0)}
+    for n in range(4):
+        hooks[PAIRS + 1 + 2 * n] = functools.partial(own_share, 0, n)
+    attend([2 * j + s for s in range(2) for j in range(PAIRS)], hooks)
+    finish(1)
+    o_copy(0).wait_recv()
+    for n in range(4):
+        own_share(1, n)
+    for n in range(4):
+        other_share(0, n)
+    o_copy(1).wait_recv()
+    for n in range(4):
+        other_share(1, n)
 
     to_mate.wait_send()
     for c in sends:
@@ -324,6 +344,7 @@
                 pltpu.VMEM((STEPS, 8, 512), F32),
                 pltpu.VMEM((256, 2048), BF),
                 pltpu.VMEM((256, HALF), BF),
+                pltpu.VMEM((256, 2048), F32),
                 dma((14,)),
                 dma((4,)),
                 dma,

time: 48.6 us -> 48.2 us (level)
  no operation moved by 1% of the time
where the time goes in v3:
time: 48.2 us; the launch traced here: 48.1 us
  Pallas kernels  47.2 us (98%)
  local copies, waits for them, and re-layouts  0.97 us (2%)
    pallas_call x1, Pallas kernels, per_device(): pl.pallas_call(lambda *refs: pl.run_scoped(functools.partial(kernel, *ref...  47.2 us
    unnamed x1, local copies, waits for them, and re-layouts  0.97 us

profile of v3, /device:TPU:0, one launch (start us, length us, event | category | flops | bytes accessed | tf_op | source)
XLA Modules:
  0.0 48.1 jit_solution(8316187299885703046)
XLA Ops:
  0.0 47.2 %attention.1 = bf16[256,2048]{1,0:T(8,128)(2,1)S(1)} custom-call(bf16[256,2048]{1,0:T(8,128)(2,1)} %bitcast.9, bf16[6144,2048]{1,0:T(8,128)(2,1)} %bitcast.7, bf16[2048,2048]{1,0:T(8,128)(2,1)} %bitcast.8), custom_call_target="tpu_custom_call" | custom-call | tf_op jit(solution)/shard_map/attention/pallas_call | solution.py:329
  47.2 1.0 %copy.5 = bf16[2,128,2048]{2,1,0:T(8,128)(2,1)} copy(bf16[2,128,2048]{2,1,0:T(8,128)(2,1)S(1)} %bitcast.6) | data formatting | bytes 2097152

commit v4 on v3

--- a/solution.py
+++ b/solution.py
@@ -274,27 +274,19 @@
     for c in wo_copies:
         c.wait()
 
-    def own_share(s, n):
-        rows, lanes = slice(s * 128, s * 128 + 128), slice(n * 512, n * 512 + 512)
-        y_acc[rows, lanes] = dot(o_buf[rows, :HALF], wo[:HALF, lanes], NN)
-
     def other_share(s, n):
         rows, lanes = slice(s * 128, s * 128 + 128), slice(n * 512, n * 512 + 512)
         y_ref[rows, lanes] = (y_acc[rows, lanes] + dot(o_buf[rows, HALF:], wo[HALF:, lanes], NN)).astype(BF)
 
-    hooks = {PAIRS - 1: lambda: finish(0)}
+    attend([2 * j + s for s in range(2) for j in range(PAIRS)], {PAIRS - 1: lambda: finish(0)})
+    finish(1)
     for n in range(4):
-        hooks[PAIRS + 1 + 2 * n] = functools.partial(own_share, 0, n)
-    attend([2 * j + s for s in range(2) for j in range(PAIRS)], hooks)
-    finish(1)
-    o_copy(0).wait_recv()
-    for n in range(4):
-        own_share(1, n)
-    for n in range(4):
-        other_share(0, n)
-    o_copy(1).wait_recv()
-    for n in range(4):
-        other_share(1, n)
+        lanes = slice(n * 512, n * 512 + 512)
+        y_acc[:, lanes] = dot(o_buf[:, :HALF], wo[:HALF, lanes], NN)
+    for s in range(2):
+        o_copy(s).wait_recv()
+        for n in range(4):
+            other_share(s, n)
 
     to_mate.wait_send()
     for c in sends:

time: 48.2 us -> 48.5 us (level)
  no operation moved by 1% of the time
where the time goes in v4:
time: 48.5 us; the launch traced here: 48.4 us
  Pallas kernels  47.4 us (98%)
  local copies, waits for them, and re-layouts  0.97 us (2%)
    pallas_call x1, Pallas kernels, per_device(): pl.pallas_call(lambda *refs: pl.run_scoped(functools.partial(kernel, *ref...  47.4 us
    unnamed x1, local copies, waits for them, and re-layouts  0.97 us

profile of v4, /device:TPU:0, one launch (start us, length us, event | category | flops | bytes accessed | tf_op | source)
XLA Modules:
  0.0 48.4 jit_solution(15833059755512485098)
XLA Ops:
  0.0 47.4 %attention.1 = bf16[256,2048]{1,0:T(8,128)(2,1)S(1)} custom-call(bf16[256,2048]{1,0:T(8,128)(2,1)} %bitcast.9, bf16[6144,2048]{1,0:T(8,128)(2,1)} %bitcast.7, bf16[2048,2048]{1,0:T(8,128)(2,1)} %bitcast.8), custom_call_target="tpu_custom_call" | custom-call | tf_op jit(solution)/shard_map/attention/pallas_call | solution.py:321
  47.4 1.0 %copy.5 = bf16[2,128,2048]{2,1,0:T(8,128)(2,1)} copy(bf16[2,128,2048]{2,1,0:T(8,128)(2,1)S(1)} %bitcast.6) | data formatting | bytes 2097152
